TPU v7x, 8 devices: a whole 2x2x1 slice. The times are simulated.
8 devices in a mesh: ens: 2 (over z, y), feat: 4 (over x, core).
Axes of the slice: x: 2, y: 2, z: 1, core: 2. Of those that a mesh axis runs over, the one named last changes fastest.
Arguments:
- particles: float32 [768, 16384], P('ens', 'feat'), parts along dimension 0
- prec_diag: float32 [32768], P(('ens', 'feat')), parts along dimension 0
- low_factor: bfloat16 [32768, 16], P(('ens', 'feat')), parts along dimension 0
- prior_mean: float32 [32768], P(('ens', 'feat')), parts along dimension 0
- data_mat: bfloat16 [1536, 16384], P('ens', 'feat'), parts along dimension 0
- labels: int32 [1536], P('ens'), parts along dimension 0
Outputs:
- output: float32 [768, 16384], P('ens', 'feat'), parts along dimension 0
There are 2 independent parts. A program takes and returns all parts, laid end to end along the dimension named above; each array names one.
All inputs are finite; a program needn't handle non-finite values.
Results may differ from a plain program's by a relative error of at most 0.001.
Values are sent between devices in bfloat16 or wider.
A program may use at most 1 GiB of HBM per device.

v0:
```python
import math
import jax
import jax.numpy as jnp
from jax import lax
from jax.sharding import PartitionSpec as P

NUM_STEPS = 3
DIMS_NT = (((1,), (1,)), ((), ()))


def solution(mesh):
    feat_size = mesh.shape["feat"]

    def local_run(particles, prec_diag, low_factor, prior_mean, data_mat, labels):
        n_part, dim_local = particles.shape
        dim_full = dim_local * feat_size
        m_rows = data_mat.shape[0]
        band_width = 2.0 * dim_full
        step_size = dim_full / 4.0
        lik_weight = 2.0 / math.sqrt(m_rows * dim_full)
        targets = labels.astype(jnp.float32)[None, :]
        state = particles
        for step_idx in range(NUM_STEPS):
            part_bf = state.astype(jnp.bfloat16)
            centred = state - prior_mean
            projected = lax.psum(jnp.dot(centred.astype(jnp.bfloat16), low_factor, preferred_element_type=jnp.float32), "feat")
            gram_mat = lax.psum(lax.dot_general(part_bf, part_bf, DIMS_NT, preferred_element_type=jnp.float32), "feat")
            logits = lax.psum(lax.dot_general(part_bf, data_mat, DIMS_NT, preferred_element_type=jnp.float32), "feat")
            sq_norm = jnp.diagonal(gram_mat)
            sq_dist = jnp.maximum(sq_norm[:, None] + sq_norm[None, :] - 2.0 * gram_mat, 0.0)
            kernel = jnp.exp(-sq_dist / band_width)
            residual = targets - jax.nn.sigmoid(logits)
            low_rank = lax.dot_general(projected.astype(jnp.bfloat16), low_factor, DIMS_NT, preferred_element_type=jnp.float32)
            lik_term = jnp.dot(residual.astype(jnp.bfloat16), data_mat, preferred_element_type=jnp.float32)
            log_grad = lik_weight * lik_term - centred * prec_diag - low_rank
            kern_bf = kernel.astype(jnp.bfloat16)
            driving = jnp.dot(kern_bf, log_grad.astype(jnp.bfloat16), preferred_element_type=jnp.float32)
            pulled = jnp.dot(kern_bf, part_bf, preferred_element_type=jnp.float32)
            row_sum = jnp.sum(kernel, axis=1, keepdims=True)
            update_dir = (driving + (2.0 / band_width) * (row_sum * state - pulled)) / n_part
            state = state + step_size * update_dir
        return state

    return jax.shard_map(
        local_run,
        mesh=mesh,
        in_specs=(P("ens", "feat"), P(("ens", "feat")), P(("ens", "feat"), None),
                  P(("ens", "feat")), P("ens", "feat"), P("ens")),
        out_specs=P("ens", "feat"),
        check_vma=False,
    )
```

profile of v0, /device:TPU:0, one launch (start us, length us, event | category | flops | bytes accessed | tf_op | source)
XLA Modules:
  0.0 287.1 jit_solution(9537383473326895166)
XLA Ops:
  6.5 7.4 %fusion.49 = f32[384,384]{1,0:T(8,128)} fusion(f32[384,4096]{1,0:T(8,128)} %param.6), kind=kOutput, calls=%fused_computation.65 | convolution fusion | flops 1209532416 | bytes 6881280 | tf_op jit(solution)/shard_map/dot_general | solution.py:27
  13.9 6.5 %fusion.47 = f32[384,768]{1,0:T(8,128)} fusion(bf16[768,4096]{1,0:T(8,128)(2,1)} %param.10, f32[384,4096]{1,0:T(8,128)S(1)} %copy-done.3), kind=kOutput, calls=%fused_computation.63 | convolution fusion | flops 2417491968 | bytes 13762560 | tf_op jit(solution)/shard_map/dot_general | solution.py:28
  20.5 0.0 all-reduce.9.cloned.1.call-start
  20.6 3.7 %fusion = f32[384,16]{1,0:T(8,128)S(1)} fusion(bf16[4096,16]{0,1:T(8,128)(2,1)S(1)} %copy-done, f32[384,4096]{1,0:T(8,128)} %param.6, f32[4096]{0:T(1024)S(1)} %copy-done.7), kind=kOutput, calls=%fused_computation.12 | convolution fusion | flops 53477376 | bytes 6463488 | tf_op jit(solution)/shard_map/dot_general | solution.py:26
  24.3 20.1 %psum.65 = bf16[384,16]{1,0:T(8,128)(2,1)S(1)} all-reduce(f32[384,16]{1,0:T(8,128)S(1)} %fusion), channel_id=1, replica_groups=mesh['ens'=2,'feat'=4] {'feat'}, use_global_device_ids=true, to_apply=%region_2.0 | all-reduce | flops 6144 | bytes 36864 | tf_op jit(solution)/shard_map/psum | solution.py:26
  44.4 22.6 %all-reduce.11.cloned.1.call-done = (f32[384,768]{1,0:T(8,128)}, f32[384,384]{1,0:T(8,128)}) async-done(((f32[384,768]{1,0:T(8,128)}, f32[384,384]{1,0:T(8,128)}), (f32[384,768]{1,0:T(8,128)}, f32[384,384]{1,0:T(8,128)})) %all-reduce.11.cloned.1.call-update) | async-done | bytes 1769488 | tf_op jit(solution)/shard_map/psum | solution.py:28
  67.0 6.5 %gather_fusion = f32[384]{0:T(512)S(1)} fusion(f32[384,384]{1,0:T(8,128)} %get-tuple-element.10, s32[384]{0:T(512)S(1)} %or_reduce_fusion), kind=kCustom, calls=%fused_computation | custom fusion | bytes 6144 | tf_op jit(solution)/shard_map/jit(diagonal)/cond/branch_0_fun/gather | solution.py:29
  73.4 1.4 fusion.18
  74.8 8.5 %fusion.9 = f32[384,4096]{1,0:T(8,128)} fusion(bf16[768,4096]{1,0:T(8,128)(2,1)} %param.10, f32[384,768]{1,0:T(8,128)} %get-tuple-element.9, f32[768]{0:T(1024)S(1)} %convert_element_type.59), kind=kOutput, calls=%fused_computation.24 | convolution fusion | flops 2417393664 | bytes 13765632 | tf_op jit(solution)/shard_map/dot_general | solution.py:34
  83.4 10.4 %fusion.6 = f32[384,4096]{1,0:T(8,128)} fusion(f32[384,4096]{1,0:T(8,128)} %fusion.9, bf16[4096,16]{0,1:T(8,128)(2,1)S(1)} %copy-done, f32[384,4096]{1,0:T(8,128)} %param.6, f32[4096]{0:T(1024)S(1)} %copy-done.8, f32[4096]{0:T(1024)S(1)} %copy-done.7, bf16[384,16]{1,0:T(8,128)(2,1)S(1)} %psum.65, f32[384,384]{1,0:T(8,128)S(1)} %copy-done.4, ...), kind=kOutput, calls=%fused_computation.18 | convolution fusion | flops 1268760576 | bytes 19641856 | tf_op jit(solution)/shard_map/dot_general | solution.py:37
  93.7 9.9 %multiply_add_fusion.2 = f32[384,4096]{1,0:T(8,128)S(1)} fusion(f32[384,4096]{1,0:T(8,128)} %param.6, f32[384,4096]{1,0:T(8,128)} %fusion.6, f32[384]{0:T(512)S(1)} %fusion.18, f32[384,384]{1,0:T(8,128)S(1)} %copy-done.4, f32[384]{0:T(512)S(1)} %gather_fusion), kind=kOutput, calls=%fused_computation.7 | convolution fusion | flops 1220001792 | bytes 19467264 | tf_op jit(solution)/shard_map/dot_general | solution.py:38
  103.6 8.8 %fusion.36 = f32[384,768]{1,0:T(8,128)} fusion(bf16[768,4096]{1,0:T(8,128)(2,1)} %param.10, f32[384,4096]{1,0:T(8,128)S(1)} %multiply_add_fusion.2), kind=kOutput, calls=%fused_computation.52 | convolution fusion | flops 2417491968 | bytes 13762560 | tf_op jit(solution)/shard_map/dot_general | solution.py:28
  112.4 2.7 fusion.38
  115.1 0.0 all-reduce.7.cloned.1.call-start
  115.1 3.7 %fusion.1 = f32[384,16]{1,0:T(8,128)S(1)} fusion(bf16[4096,16]{0,1:T(8,128)(2,1)S(1)} %copy-done, f32[384,4096]{1,0:T(8,128)} %copy-done.2, f32[4096]{0:T(1024)S(1)} %copy-done.7), kind=kOutput, calls=%fused_computation.13 | convolution fusion | flops 53477376 | bytes 6463488 | tf_op jit(solution)/shard_map/dot_general | solution.py:26
  118.9 17.3 %psum.68 = bf16[384,16]{1,0:T(8,128)(2,1)S(1)} all-reduce(f32[384,16]{1,0:T(8,128)S(1)} %fusion.1), channel_id=1, replica_groups=mesh['ens'=2,'feat'=4] {'feat'}, use_global_device_ids=true, to_apply=%region_6.7 | all-reduce | flops 6144 | bytes 36864 | tf_op jit(solution)/shard_map/psum | solution.py:26
  136.2 22.6 %all-reduce.9.cloned.1.call-done = (f32[384,768]{1,0:T(8,128)}, f32[384,384]{1,0:T(8,128)}) async-done(((f32[384,768]{1,0:T(8,128)}, f32[384,384]{1,0:T(8,128)}), (f32[384,768]{1,0:T(8,128)}, f32[384,384]{1,0:T(8,128)})) %all-reduce.9.cloned.1.call-update) | async-done | bytes 1769488 | tf_op jit(solution)/shard_map/psum | solution.py:28
  158.8 8.5 %fusion.10 = f32[384,4096]{1,0:T(8,128)} fusion(bf16[768,4096]{1,0:T(8,128)(2,1)} %param.10, f32[384,768]{1,0:T(8,128)} %get-tuple-element.7, f32[768]{0:T(1024)S(1)} %convert_element_type.59), kind=kOutput, calls=%fused_computation.25 | convolution fusion | flops 2417393664 | bytes 13765632 | tf_op jit(solution)/shard_map/dot_general | solution.py:34
  167.3 3.4 %gather_fusion.1 = f32[384]{0:T(512)S(1)} fusion(f32[384,384]{1,0:T(8,128)S(1)} %copy-done.5, s32[384]{0:T(512)S(1)} %or_reduce_fusion), kind=kCustom, calls=%fused_computation.1 | custom fusion | bytes 6144 | tf_op jit(solution)/shard_map/jit(diagonal)/cond/branch_0_fun/gather | solution.py:29
  170.8 0.3 fusion.20
  171.1 10.4 %fusion.7 = f32[384,4096]{1,0:T(8,128)} fusion(f32[384,4096]{1,0:T(8,128)} %fusion.10, bf16[4096,16]{0,1:T(8,128)(2,1)S(1)} %copy-done, f32[384,4096]{1,0:T(8,128)} %copy-done.2, f32[4096]{0:T(1024)S(1)} %copy-done.8, f32[4096]{0:T(1024)S(1)} %copy-done.7, bf16[384,16]{1,0:T(8,128)(2,1)S(1)} %psum.68, f32[384,384]{1,0:T(8,128)S(1)} %copy-done.5, ...), kind=kOutput, calls=%fused_computation.19 | convolution fusion | flops 1268760576 | bytes 19641856 | tf_op jit(solution)/shard_map/dot_general | solution.py:37
  181.5 9.8 %multiply_add_fusion.1 = f32[384,4096]{1,0:T(8,128)S(1)} fusion(f32[384,4096]{1,0:T(8,128)} %copy-done.2, f32[384,4096]{1,0:T(8,128)} %fusion.7, f32[384]{0:T(512)S(1)} %fusion.20, f32[384,384]{1,0:T(8,128)S(1)} %copy-done.5, f32[384]{0:T(512)S(1)} %gather_fusion.1), kind=kOutput, calls=%fused_computation.5 | convolution fusion | flops 1220001792 | bytes 19467264 | tf_op jit(solution)/shard_map/dot_general | solution.py:38
  191.3 8.8 %fusion.31 = f32[384,768]{1,0:T(8,128)} fusion(bf16[768,4096]{1,0:T(8,128)(2,1)} %param.10, f32[384,4096]{1,0:T(8,128)S(1)} %multiply_add_fusion.1), kind=kOutput, calls=%fused_computation.47 | convolution fusion | flops 2417491968 | bytes 13762560 | tf_op jit(solution)/shard_map/dot_general | solution.py:28
  200.1 2.7 fusion.33
  202.8 3.7 %fusion.2 = f32[384,16]{1,0:T(8,128)S(1)} fusion(bf16[4096,16]{0,1:T(8,128)(2,1)S(1)} %copy-done, f32[384,4096]{1,0:T(8,128)} %copy-done.1, f32[4096]{0:T(1024)S(1)} %copy-done.7), kind=kOutput, calls=%fused_computation.14 | convolution fusion | flops 53477376 | bytes 6463488 | tf_op jit(solution)/shard_map/dot_general | solution.py:26
  206.6 17.4 %psum.71 = bf16[384,16]{1,0:T(8,128)(2,1)S(1)} all-reduce(f32[384,16]{1,0:T(8,128)S(1)} %fusion.2), channel_id=1, replica_groups=mesh['ens'=2,'feat'=4] {'feat'}, use_global_device_ids=true, to_apply=%region_10.11 | all-reduce | flops 6144 | bytes 36864 | tf_op jit(solution)/shard_map/psum | solution.py:26
  223.9 22.6 %all-reduce.7.cloned.1.call-done = (f32[384,768]{1,0:T(8,128)}, f32[384,384]{1,0:T(8,128)}) async-done(((f32[384,768]{1,0:T(8,128)}, f32[384,384]{1,0:T(8,128)}), (f32[384,768]{1,0:T(8,128)}, f32[384,384]{1,0:T(8,128)})) %all-reduce.7.cloned.1.call-update) | async-done | bytes 1769488 | tf_op jit(solution)/shard_map/psum | solution.py:28
  246.5 8.5 %fusion.11 = f32[384,4096]{1,0:T(8,128)} fusion(bf16[768,4096]{1,0:T(8,128)(2,1)} %param.10, f32[384,768]{1,0:T(8,128)} %get-tuple-element.5, f32[768]{0:T(1024)S(1)} %convert_element_type.59), kind=kOutput, calls=%fused_computation.26 | convolution fusion | flops 2417393664 | bytes 13765632 | tf_op jit(solution)/shard_map/dot_general | solution.py:34
  255.1 3.4 %gather_fusion.2 = f32[384]{0:T(512)S(1)} fusion(f32[384,384]{1,0:T(8,128)S(1)} %copy-done.6, s32[384]{0:T(512)S(1)} %or_reduce_fusion), kind=kCustom, calls=%fused_computation.2 | custom fusion | bytes 6144 | tf_op jit(solution)/shard_map/jit(diagonal)/cond/branch_0_fun/gather | solution.py:29
  258.5 0.3 fusion.22
  258.8 10.4 %fusion.8 = f32[384,4096]{1,0:T(8,128)} fusion(f32[384,4096]{1,0:T(8,128)} %fusion.11, bf16[4096,16]{0,1:T(8,128)(2,1)S(1)} %copy-done, f32[384,4096]{1,0:T(8,128)} %copy-done.1, f32[4096]{0:T(1024)S(1)} %copy-done.8, f32[4096]{0:T(1024)S(1)} %copy-done.7, bf16[384,16]{1,0:T(8,128)(2,1)S(1)} %psum.71, f32[384,384]{1,0:T(8,128)S(1)} %copy-done.6, ...), kind=kOutput, calls=%fused_computation.20 | convolution fusion | flops 1268760576 | bytes 19641856 | tf_op jit(solution)/shard_map/dot_general | solution.py:37
  269.2 11.4 %multiply_add_fusion = f32[384,4096]{1,0:T(8,128)} fusion(f32[384,4096]{1,0:T(8,128)} %copy-done.1, f32[384,4096]{1,0:T(8,128)} %fusion.8, f32[384]{0:T(512)S(1)} %fusion.22, f32[384,384]{1,0:T(8,128)S(1)} %copy-done.6, f32[384]{0:T(512)S(1)} %gather_fusion.2), kind=kOutput, calls=%fused_computation.3 | convolution fusion | flops 1220001792 | bytes 19467264 | tf_op jit(solution)/shard_map/dot_general | solution.py:38
  (26 shorter events, 0.1 us)
Async XLA Ops:
  6.5 14.1 %copy-start = (bf16[4096,16]{0,1:T(8,128)(2,1)S(1)}, bf16[4096,16]{0,1:T(8,128)(2,1)}, u32[]{:S(2)}) copy-start(bf16[4096,16]{0,1:T(8,128)(2,1)} %param.8) | copy-start | bytes 393220
  6.5 60.4 %all-reduce.11.cloned.1.call-start = ((), (), s32[]{:S(2)}) async-start(), calls=%async_computation.2 | async-start | bytes 3538944 | tf_op jit(solution)/shard_map/psum | solution.py:28
  6.5 7.4 %copy-start.3 = (f32[384,4096]{1,0:T(8,128)S(1)}, f32[384,4096]{1,0:T(8,128)}, u32[]{:S(2)}) copy-start(f32[384,4096]{1,0:T(8,128)} %param.6) | copy-start | bytes 18874372
  13.9 6.6 %copy-start.9 = (s32[768]{0:T(1024)S(1)}, s32[768]{0:T(1024)}, u32[]{:S(2)}) copy-start(s32[768]{0:T(1024)} %param.11) | copy-start | bytes 9220
  13.9 6.7 %copy-start.7 = (f32[4096]{0:T(1024)S(1)}, f32[4096]{0:T(1024)}, u32[]{:S(2)}) copy-start(f32[4096]{0:T(1024)} %param.9) | copy-start | bytes 49156
  20.5 138.3 %all-reduce.9.cloned.1.call-start = ((), (), s32[]{:S(2)}) async-start(), calls=%async_computation.1 | async-start | bytes 3538944 | tf_op jit(solution)/shard_map/psum | solution.py:28
  74.8 8.6 %copy-start.4 = (f32[384,384]{1,0:T(8,128)S(1)}, f32[384,384]{1,0:T(8,128)}, u32[]{:S(2)}) copy-start(f32[384,384]{1,0:T(8,128)} %get-tuple-element.10) | copy-start | bytes 1769476
  74.8 8.6 %copy-start.8 = (f32[4096]{0:T(1024)S(1)}, f32[4096]{0:T(1024)}, u32[]{:S(2)}) copy-start(f32[4096]{0:T(1024)} %param.7) | copy-start | bytes 49156
  103.6 8.8 %copy-start.2 = (f32[384,4096]{1,0:T(8,128)}, f32[384,4096]{1,0:T(8,128)S(1)}, u32[]{:S(2)}) copy-start(f32[384,4096]{1,0:T(8,128)S(1)} %multiply_add_fusion.2) | copy-start | bytes 18874372
  115.1 131.4 %all-reduce.7.cloned.1.call-start = ((), (), s32[]{:S(2)}) async-start(), calls=%async_computation | async-start | bytes 3538944 | tf_op jit(solution)/shard_map/psum | solution.py:28
  158.8 8.5 %copy-start.5 = (f32[384,384]{1,0:T(8,128)S(1)}, f32[384,384]{1,0:T(8,128)}, u32[]{:S(2)}) copy-start(f32[384,384]{1,0:T(8,128)} %get-tuple-element.8) | copy-start | bytes 1769476
  191.3 8.8 %copy-start.1 = (f32[384,4096]{1,0:T(8,128)}, f32[384,4096]{1,0:T(8,128)S(1)}, u32[]{:S(2)}) copy-start(f32[384,4096]{1,0:T(8,128)S(1)} %multiply_add_fusion.1) | copy-start | bytes 18874372
  246.5 8.5 %copy-start.6 = (f32[384,384]{1,0:T(8,128)S(1)}, f32[384,384]{1,0:T(8,128)}, u32[]{:S(2)}) copy-start(f32[384,384]{1,0:T(8,128)} %get-tuple-element.6) | copy-start | bytes 1769476
Sparse Core Ops, SparseCore 0:
  20.6 46.3 all-reduce.10
  115.2 43.5 all-reduce.8
  202.9 43.5 all-reduce.6
where the time goes:
time: 288 us; the launch traced here: 287 us
  matrix products  136 us (47%)
  waiting for transfers between devices  67.7 us (24%)
  blocking collectives  54.8 us (19%)
  local copies, waits for them, and re-layouts  13.4 us (5%)
  between operations  13.3 us (5%)
    psum x3, waiting for transfers between devices, local_run(): lax.psum(lax.dot_general(part_bf, data_mat, DIMS_NT, preferred_element_ty...  67.7 us
    psum x3, blocking collectives, local_run(): lax.psum(jnp.dot(centred.astype(jnp.bfloat16), low_factor, preferred_elem...  54.8 us
    dot_general x3, matrix products, local_run(): jnp.dot(kern_bf, log_grad.astype(jnp.bfloat16), preferred_element_type=jn...  31.1 us
    dot_general x3, matrix products, local_run(): pulled = jnp.dot(kern_bf, part_bf, preferred_element_type=jnp.float32)  31.1 us
    dot_general x3, matrix products, local_run(): jnp.dot(residual.astype(jnp.bfloat16), data_mat, preferred_element_type=j...  25.6 us
    dot_general x3, matrix products, local_run(): lax.dot_general(part_bf, data_mat, DIMS_NT, preferred_element_type=jnp.fl...  24.1 us
    gather x3, local copies, waits for them, and re-layouts, local_run(): sq_norm = jnp.diagonal(gram_mat)  13.3 us
    dot_general x3, matrix products, local_run(): lax.dot_general(part_bf, part_bf, DIMS_NT, preferred_element_type=jnp.flo...  12.7 us
  transfers between devices with their start and end apart: 3, of which 3 were waited for; matrix products, arithmetic and copies ran while one was open for 4% of the time, Pallas kernels for 0%

commit v1 on v0

v1 whole, which is shorter than its diff:
```python
import functools
import math

import jax
import jax.numpy as jnp
from jax import lax
from jax.experimental import pallas as pl
from jax.experimental.pallas import tpu as pltpu
from jax.sharding import PartitionSpec as P

NUM_STEPS = 3
DIMS_NT = (((1,), (1,)), ((), ()))
MESH = pl.DeviceIdType.MESH
F32 = jnp.float32
BF16 = jnp.bfloat16

NP = 384
MD = 768
CH = 256
NC = MD // CH
OWN = NP // 4
PH = 328
BF = 512

D2D_Z, ICI_Z, ICI_R, D2D_R, D2D_F = 0, NC, 2 * NC, 3 * NC, 4 * NC
D2D_P = 5 * NC
ICI_P, D2D_PG, D2D_Q, ICI_Q, D2D_QG = (D2D_P + i for i in range(1, 6))
N_SEM = D2D_P + 6


def kernel(beta, c1, c2, inv_h, th_hbm, lam, mu, u, a_hbm, y, out_hbm,
           th, a, tb, base, zp, zr1, zr2, rb, pp, pr1, pr2, pf, qp, qr1, qr2, qf,
           kb, krow, qb, ss, rs, ls):
    dim = th.shape[1]
    nb = dim // BF
    me = lax.axis_index("feat")
    x, core = lax.div(me, 2), lax.rem(me, 2)
    ox, oc = 1 - x, 1 - core
    partner, cross = x * 2 + oc, ox * 2 + core

    def remote(src, dst, slot, dev):
        return pltpu.make_async_remote_copy(
            src_ref=src, dst_ref=dst, send_sem=ss.at[slot], recv_sem=rs.at[slot],
            device_id={"feat": dev}, device_id_type=MESH)

    def cols(b):
        return pl.ds(pl.multiple_of(b * BF, BF), BF)

    def th_load(b):
        return pltpu.make_async_copy(th_hbm.at[:, cols(b)], th.at[:, cols(b)], ls.at[b])

    def a_load(c):
        return pltpu.make_async_copy(a_hbm.at[pl.ds(c * CH, CH)], a.at[pl.ds(c * CH, CH)], ls.at[nb + c])

    def out_store(b):
        return pltpu.make_async_copy(th.at[:, cols(b)], out_hbm.at[:, cols(b)], ls.at[nb + NC + b])

    for b in range(nb):
        th_load(b).start()
    for c in range(NC):
        a_load(c).start()

    barrier = pltpu.get_barrier_semaphore()
    for dev in (partner, cross):
        pl.semaphore_signal(barrier, inc=1, device_id={"feat": dev}, device_id_type=MESH)
    pl.semaphore_wait(barrier, 2)

    def conv(b, carry):
        th_load(b).wait()
        tb[:, cols(b)] = th[:, cols(b)].astype(BF16)
        return carry

    lax.fori_loop(0, nb, conv, 0)
    for c in range(NC):
        a_load(c).wait()

    rows_i = lax.broadcasted_iota(jnp.int32, (128, 128), 0)
    cols_i = lax.broadcasted_iota(jnp.int32, (128, 128), 1)

    def step_body(step, carry):
        d2d_z = [remote(zp.at[c, oc], zr1.at[c], D2D_Z + c, partner) for c in range(NC)]
        ici_z = [remote(zp.at[c, core, ox], zr2.at[c], ICI_Z + c, cross) for c in range(NC)]
        ici_r = [remote(rb.at[c, core, x], rb.at[c, core, x], ICI_R + c, cross) for c in range(NC)]
        d2d_r = [remote(rb.at[c, core, x], rb.at[c, core, x], D2D_R + c, partner) for c in range(NC)]
        d2d_f = [remote(rb.at[c, core, ox], rb.at[c, core, ox], D2D_F + c, partner) for c in range(NC)]
        d2d_p = remote(pp.at[oc], pr1, D2D_P, partner)
        ici_p = remote(pp.at[core], pr2, ICI_P, cross)
        d2d_pg = remote(pf.at[core], pf.at[core], D2D_PG, partner)
        d2d_q = remote(qp.at[oc], qr1, D2D_Q, partner)
        ici_q = remote(qp.at[core], qr2, ICI_Q, cross)
        d2d_qg = remote(qf.at[core], qf.at[core], D2D_QG, partner)

        def z_dot(c):
            z = lax.dot_general(tb[...], a[pl.ds(c * CH, CH), :], DIMS_NT, preferred_element_type=F32)
            zp[c] = z.reshape(2, 2, OWN, CH)
            d2d_z[c].start()

        def z_chip(c):
            d2d_z[c].wait_recv()
            zp[c, core] = zp[c, core] + zr1[c].reshape(2, OWN, CH)
            ici_z[c].start()

        def r_own(c):
            ici_z[c].wait_recv()
            z = zp[c, core, x] + zr2[c]
            r = y[:, pl.ds(c * CH, CH)].astype(F32) - jax.nn.sigmoid(z)
            rb[c, core, x] = r.astype(BF16)
            ici_r[c].start()
            d2d_r[c].start()

        def r_forward(c):
            ici_r[c].wait_recv()
            d2d_f[c].start()

        def r_all(c):
            d2d_r[c].wait_recv()
            d2d_f[c].wait_recv()

        z_dot(0)
        ga = lax.dot_general(tb[...], tb[0:256, :], DIMS_NT, preferred_element_type=F32)
        z_chip(0)
        d2 = lax.dot_general(tb[256:384, :], tb[256:384, :], DIMS_NT, preferred_element_type=F32)
        d0, d1 = ga[0:128, 0:128], ga[128:256, 128:256]

        def diag_row(d):
            return jnp.sum(jnp.where(rows_i == cols_i, d, 0.0), axis=0, keepdims=True)

        rid = lax.broadcasted_iota(jnp.int32, (16, 128), 0)
        diag = jnp.where(rid == 0, diag_row(d0), jnp.where(rid == 1, diag_row(d1), diag_row(d2)))
        packed = jnp.concatenate(
            [ga[128:256, 0:128], ga[256:384, 0:128], ga[256:384, 128:256],
             jnp.where(rows_i >= cols_i, d0, d1), d2, diag], axis=0)
        pp[0] = packed[0:PH]
        pp[1] = packed[PH:2 * PH]
        d2d_p.start()

        z_dot(1)
        d2d_p.wait_recv()
        pp[core] = pp[core] + pr1[...]
        ici_p.start()

        def q_block(b, acc):
            xb = (th[:, cols(b)] - mu[:, cols(b)]).astype(BF16)
            return acc + jnp.dot(xb, u[pl.ds(pl.multiple_of(b * BF, BF), BF), :], preferred_element_type=F32)

        q = lax.fori_loop(0, nb, q_block, jnp.zeros((NP, 16), F32))
        qp[...] = q.T.reshape(2, 8, NP)
        d2d_q.start()

        z_dot(2)
        d2d_q.wait_recv()
        qp[core] = qp[core] + qr1[...]
        ici_q.start()
        z_chip(1)
        z_chip(2)
        r_own(0)

        ici_p.wait_recv()
        pf[core] = pp[core] + pr2[...]
        d2d_pg.start()
        ici_q.wait_recv()
        qf[core] = qp[core] + qr2[...]
        d2d_qg.start()
        d2d_pg.wait_recv()

        full = pf[...].reshape(2 * PH, 128)
        n_row = [full[640 + i:641 + i, :] for i in range(3)]
        n_col = [jnp.sum(jnp.where(rows_i == cols_i, n, 0.0), axis=1, keepdims=True) for n in n_row]

        def kern(ni, nj, g):
            return jnp.exp(-(jnp.maximum(ni + nj - 2.0 * g, 0.0) * inv_h))

        k10 = kern(n_col[1], n_row[0], full[0:128])
        k20 = kern(n_col[2], n_row[0], full[128:256])
        k21 = kern(n_col[2], n_row[1], full[256:384])
        low = rows_i >= cols_i
        kmix = kern(jnp.where(low, n_col[0], n_col[1]), jnp.where(low, n_row[0], n_row[1]), full[384:512])
        k22 = kern(n_col[2], n_row[2], full[512:640])
        kmix_t = kmix.T
        k00 = jnp.where(low, kmix, kmix_t)
        k11 = jnp.where(rows_i < cols_i, kmix, jnp.where(rows_i > cols_i, kmix_t, 1.0))
        kmat = [[k00, k10.T, k20.T], [k10, k11, k21.T], [k20, k21, k22]]
        for i in range(3):
            for j in range(3):
                kb[128 * i:128 * (i + 1), 128 * j:128 * (j + 1)] = kmat[i][j].astype(BF16)
            k_sum = jnp.sum(kmat[i][0] + kmat[i][1] + kmat[i][2], axis=1, keepdims=True)
            krow[128 * i:128 * (i + 1), :] = jnp.broadcast_to(k_sum, (128, 128))

        d2d_qg.wait_recv()
        qb[...] = qf[...].reshape(16, NP).T.astype(BF16)

        r_own(1)

        def base_block(b, carry):
            t = th[:, cols(b)]
            low_rank = lax.dot_general(qb[...], u[pl.ds(pl.multiple_of(b * BF, BF), BF), :], DIMS_NT,
                                       preferred_element_type=F32)
            base[:, cols(b)] = -((t - mu[:, cols(b)]) * lam[:, cols(b)]) - low_rank
            pulled = jnp.dot(kb[...], tb[:, cols(b)], preferred_element_type=F32)
            th[:, cols(b)] = t + c1 * (krow[:, 0:1] * t - pulled)
            return carry

        lax.fori_loop(0, nb // 2, base_block, 0)
        r_own(2)
        lax.fori_loop(nb // 2, nb, base_block, 0)

        def ra_chunk(c):
            def ra_block(b, carry):
                ra = jnp.dot(rb[c].reshape(NP, CH), a[pl.ds(c * CH, CH), cols(b)], preferred_element_type=F32)
                base[:, cols(b)] = base[:, cols(b)] + beta * ra
                return carry
            lax.fori_loop(0, nb, ra_block, 0)

        r_forward(0)
        r_forward(1)
        r_all(0)
        ra_chunk(0)
        r_forward(2)
        r_all(1)
        ra_chunk(1)
        r_all(2)

        def final_block(b, carry):
            c = NC - 1
            ra = jnp.dot(rb[c].reshape(NP, CH), a[pl.ds(c * CH, CH), cols(b)], preferred_element_type=F32)
            s = (base[:, cols(b)] + beta * ra).astype(BF16)
            t = th[:, cols(b)] + c2 * jnp.dot(kb[...], s, preferred_element_type=F32)
            th[:, cols(b)] = t
            tb[:, cols(b)] = t.astype(BF16)

            @pl.when(step == NUM_STEPS - 1)
            def _():
                out_store(b).start()
            return carry

        lax.fori_loop(0, nb, final_block, 0)

        for cp in d2d_z + ici_z + ici_r + d2d_r + d2d_f + [d2d_p, ici_p, d2d_pg, d2d_q, ici_q, d2d_qg]:
            cp.wait_send()
        return carry

    lax.fori_loop(0, NUM_STEPS, step_body, 0)
    for b in range(nb):
        out_store(b).wait()


def solution(mesh):
    feat_size = mesh.shape["feat"]

    def local_run(particles, prec_diag, low_factor, prior_mean, data_mat, labels):
        n_part, dim_local = particles.shape
        dim_full = dim_local * feat_size
        m_rows = data_mat.shape[0]
        band_width = 2.0 * dim_full
        step_size = dim_full / 4.0
        beta = 2.0 / math.sqrt(m_rows * dim_full)
        c1 = step_size * (2.0 / band_width) / n_part
        c2 = step_size / n_part
        nb = dim_local // BF
        vm = pltpu.VMEM
        scratch = [
            vm((NP, dim_local), F32),
            vm((MD, dim_local), BF16),
            vm((NP, dim_local), BF16),
            vm((NP, dim_local), F32),
            vm((NC, 2, 2, OWN, CH), F32),
            vm((NC, 2, OWN, CH), F32),
            vm((NC, OWN, CH), F32),
            vm((NC, 2, 2, OWN, CH), BF16),
            vm((2, PH, 128), F32),
            vm((PH, 128), F32),
            vm((PH, 128), F32),
            vm((2, PH, 128), F32),
            vm((2, 8, NP), F32),
            vm((8, NP), F32),
            vm((8, NP), F32),
            vm((2, 8, NP), F32),
            vm((NP, NP), BF16),
            vm((NP, 128), F32),
            vm((NP, 16), BF16),
            pltpu.SemaphoreType.DMA((N_SEM,)),
            pltpu.SemaphoreType.DMA((N_SEM,)),
            pltpu.SemaphoreType.DMA((2 * nb + NC,)),
        ]
        anyspec = pl.BlockSpec(memory_space=pl.ANY)
        vspec = pl.BlockSpec(memory_space=pltpu.VMEM)
        return pl.pallas_call(
            functools.partial(kernel, beta, c1, c2, 1.0 / band_width),
            out_shape=jax.ShapeDtypeStruct((n_part, dim_local), F32),
            in_specs=[anyspec, vspec, vspec, vspec, anyspec, vspec],
            out_specs=anyspec,
            scratch_shapes=scratch,
            compiler_params=pltpu.CompilerParams(
                collective_id=0, has_side_effects=True, vmem_limit_bytes=60 * 1024 * 1024),
            name="svgd",
        )(particles, prec_diag.reshape(1, dim_local), prior_mean.reshape(1, dim_local), low_factor,
          data_mat, labels.reshape(1, m_rows))

    return jax.shard_map(
        local_run,
        mesh=mesh,
        in_specs=(P("ens", "feat"), P(("ens", "feat")), P(("ens", "feat"), None),
                  P(("ens", "feat")), P("ens", "feat"), P("ens")),
        out_specs=P("ens", "feat"),
        check_vma=False,
    )
```

time: 288 us -> 103 us (0.36)
  matrix products: 136 us -> 0 us
  Pallas kernels: 0 us -> 93.1 us
  waiting for transfers between devices: 67.7 us -> 0 us
  blocking collectives: 54.8 us -> 0 us
  between operations: 13.3 us -> 0.01 us
  local copies, waits for them, and re-layouts: 13.4 us -> 9.69 us
    dot_general x18 -> x0, matrix products: 136 us -> none  [the longest x3 31.1 us: local_run(): jnp.dot(kern_bf, log_grad.astype(jnp.bfloat16), preferred_element_type=jn...]
    pallas_call x0 -> x1, Pallas kernels: none -> 93.1 us  [local_run(): pl.pallas_call(functools.partial(kernel, beta, c1, c2, 1.0 / band_width),...]
    psum x3 -> x0, waiting for transfers between devices: 67.7 us -> none  [local_run(): lax.psum(lax.dot_general(part_bf, data_mat, DIMS_NT, preferred_element_ty...]
    psum x3 -> x0, blocking collectives: 54.8 us -> none  [local_run(): lax.psum(jnp.dot(centred.astype(jnp.bfloat16), low_factor, preferred_elem...]
    gather x3 -> x0, local copies, waits for them, and re-layouts: 13.3 us -> none  [local_run(): sq_norm = jnp.diagonal(gram_mat)]
    unnamed x20 -> x2, local copies, waits for them, and re-layouts: 0.04 us -> 8.41 us
  transfers between devices with their start and end apart: 3 -> 0, of which waited for: 3 -> 0; matrix products, arithmetic and copies ran while one was open for 4% -> 0% of each run, Pallas kernels for 0% -> 0%
where the time goes in v1:
time: 103 us
  Pallas kernels  93.1 us (90%)
  local copies, waits for them, and re-layouts  9.69 us (9%)
    pallas_call x1, Pallas kernels, local_run(): pl.pallas_call(functools.partial(kernel, beta, c1, c2, 1.0 / band_width),...  93.1 us
    unnamed x2, local copies, waits for them, and re-layouts  8.41 us

profile of v1, /device:TPU:0, one launch (start us, length us, event | category | flops | bytes accessed | tf_op | source)
XLA Modules:
  0.0 102.8 jit_solution(1227150889150683250)
XLA Ops:
  0.0 1.3 %reshape.11.y = s32[1,768]{1,0:T(1,128)} reshape(s32[768]{0:T(1024)} %param.11) | data formatting | bytes 6144 | tf_op jit(solution)/shard_map/reshape | solution.py:297
  1.3 2.2 %copy.7.u = bf16[4096,16]{1,0:T(8,128)(2,1)} copy(bf16[4096,16]{0,1:T(8,128)(2,1)} %param.8) | data formatting | bytes 262144 | tf_op args[2]
  3.5 93.1 %svgd.1 = f32[384,4096]{1,0:T(8,128)} custom-call(f32[384,4096]{1,0:T(8,128)} %th_hbm.1, f32[1,4096]{1,0:T(1,128)} %bitcast.2, f32[1,4096]{1,0:T(1,128)} %bitcast.3, bf16[4096,16]{1,0:T(8,128)(2,1)} %copy.7.u, bf16[768,4096]{1,0:T(8,128)(2,1)} %a_hbm.1, s32[1,768]{1,0:T(1,128)} %reshape.11.y), custom_call_target="tpu_custom_call" | custom-call | tf_op jit(solution)/shard_map/svgd/pallas_call | solution.py:287
  96.6 6.2 %copy.9 = f32[384,4096]{1,0:T(8,128)} copy(f32[384,4096]{1,0:T(8,128)} %svgd.1) | data formatting | bytes 12582912

commit v2 on v0

v2 whole, which is shorter than its diff:
```python
import functools
import math

import jax
import jax.numpy as jnp
from jax import lax
from jax.experimental import pallas as pl
from jax.experimental.pallas import tpu as pltpu
from jax.sharding import PartitionSpec as P

NUM_STEPS = 3
DIMS_NT = (((1,), (1,)), ((), ()))
MESH = pl.DeviceIdType.MESH
F32 = jnp.float32
BF16 = jnp.bfloat16

NP = 384
MD = 768
CH = 256
NC = MD // CH
OWN = NP // 4
QR = 144
BL = 512
BQ = 4096
BB = 4096
BK = 4096
BR = 4096
BU = 4096

D2D_Z, ICI_Z, ICI_R, D2D_R, D2D_F = 0, NC, 2 * NC, 3 * NC, 4 * NC
(D2D_P, ICI_P, ICI_K, D2D_K, FWD_K, ICI_S, D2D_S, FWD_S,
 D2D_Q, ICI_Q, D2D_QG) = range(5 * NC, 5 * NC + 11)
N_SEM = 5 * NC + 11


def kernel(beta, c1, c2, two_h, inv_h, th_hbm, lam_hbm, mu_hbm, u_hbm, a_hbm, y_hbm, th,
           lam, mu, u, y, a, at, tb, base, zp, zr1, zr2, rb, pp, pr1, pr2, ns, k32, k16, ks, qp, qr1, qr2, qf,
           kb, krow, qb, ss, rs, ls):
    dim = th.shape[1]
    nb = dim // BL
    me = lax.axis_index("feat")
    x, core = lax.div(me, 2), lax.rem(me, 2)
    ox, oc = 1 - x, 1 - core
    partner, cross = x * 2 + oc, ox * 2 + oc
    h = lax.rem(x + core, 2)
    oh = 1 - h

    def remote(src, dst, slot, dev):
        return pltpu.make_async_remote_copy(
            src_ref=src, dst_ref=dst, send_sem=ss.at[slot], recv_sem=rs.at[slot],
            device_id={"feat": dev}, device_id_type=MESH)

    def cols(b, size):
        return pl.ds(pl.multiple_of(b * size, size), size)

    def th_load(b):
        return pltpu.make_async_copy(th_hbm.at[:, cols(b, BL)], th.at[:, cols(b, BL)], ls.at[b])

    def a_load(c):
        return pltpu.make_async_copy(a_hbm.at[pl.ds(c * CH, CH)], a.at[pl.ds(c * CH, CH)], ls.at[nb + c])

    small = [pltpu.make_async_copy(src, dst, ls.at[nb + NC + i])
             for i, (src, dst) in enumerate([(lam_hbm, lam), (mu_hbm, mu), (u_hbm, u), (y_hbm, y)])]
    for b in range(nb):
        th_load(b).start()
    for c in range(NC):
        a_load(c).start()
    for cp in small:
        cp.start()

    barrier = pltpu.get_barrier_semaphore()
    for dev in (partner, cross):
        pl.semaphore_signal(barrier, inc=1, device_id={"feat": dev}, device_id_type=MESH)
    pl.semaphore_wait(barrier, 2)

    k32[...] = jnp.zeros_like(k32)

    def conv(b, carry):
        th_load(b).wait()
        tb[:, cols(b, BL)] = th[:, cols(b, BL)].astype(BF16)
        return carry

    lax.fori_loop(0, nb, conv, 0)
    for cp in small:
        cp.wait()

    ri = lax.broadcasted_iota(jnp.int32, (128, 128), 0)
    ci = lax.broadcasted_iota(jnp.int32, (128, 128), 1)
    eye, low = ri == ci, ri >= ci
    r64 = lax.broadcasted_iota(jnp.int32, (64, 128), 0)
    c64 = lax.broadcasted_iota(jnp.int32, (64, 128), 1)
    fold = (c64 < 64) & (r64 < c64)
    straight = ((ri < 64) & ((ci >= 64) | low)) | ((ri >= 64) & (ci > ri))
    r8 = lax.broadcasted_iota(jnp.int32, (8, 128), 0)

    def rows3(v):
        return jnp.where(r8 == 0, v[0], jnp.where(r8 == 1, v[1], jnp.where(r8 == 2, v[2], 0.0)))

    def to_col(row):
        return jnp.sum(jnp.where(eye, row, 0.0), axis=1, keepdims=True)

    def unpack(p, one):
        m10, m20, m21, mix, m2 = p[0:128], p[128:256], p[256:384], p[384:512], p[512:576]
        mix_t = mix.T
        d0 = jnp.where(low, mix, mix_t)
        d1 = jnp.where(ri < ci, mix, jnp.where(eye, one, mix_t))
        f = jnp.concatenate([m2, pltpu.roll(m2, 64, 1)], axis=0)
        d2 = jnp.where(straight, f, jnp.where(eye & (ri >= 64), one, f.T))
        return [[d0, m10.T, m20.T], [m10, d1, m21.T], [m20, m21, d2]]

    def step_body(step, carry):
        d2d_z = [remote(zp.at[c, oh], zr1.at[c], D2D_Z + c, partner) for c in range(NC)]
        ici_z = [remote(zp.at[c, h, ox], zr2.at[c], ICI_Z + c, cross) for c in range(NC)]
        ici_r = [remote(rb.at[c, h, x], rb.at[c, h, x], ICI_R + c, cross) for c in range(NC)]
        d2d_r = [remote(rb.at[c, h, x], rb.at[c, h, x], D2D_R + c, partner) for c in range(NC)]
        d2d_f = [remote(rb.at[c, h, ox], rb.at[c, h, ox], D2D_F + c, partner) for c in range(NC)]
        d2d_p = remote(pp.at[oh], pr1, D2D_P, partner)
        ici_p = remote(pp.at[h, ox], pr2, ICI_P, cross)
        ici_k = remote(k16.at[h, x], k16.at[h, x], ICI_K, cross)
        d2d_k = remote(k16.at[h, x], k16.at[h, x], D2D_K, partner)
        fwd_k = remote(k16.at[h, ox], k16.at[h, ox], FWD_K, partner)
        ici_s = remote(ks.at[h, x], ks.at[h, x], ICI_S, cross)
        d2d_s = remote(ks.at[h, x], ks.at[h, x], D2D_S, partner)
        fwd_s = remote(ks.at[h, ox], ks.at[h, ox], FWD_S, partner)
        d2d_q = remote(qp.at[oh], qr1, D2D_Q, partner)
        ici_q = remote(qp.at[h], qr2, ICI_Q, cross)
        d2d_qg = remote(qf.at[h], qf.at[h], D2D_QG, partner)

        def z_dot(c):
            @pl.when(step == 0)
            def _():
                a_load(c).wait()
                z = lax.dot_general(tb[...], a[pl.ds(c * CH, CH), :], DIMS_NT, preferred_element_type=F32)
                zp[c] = z.reshape(2, 2, OWN, CH)

            @pl.when(step > 0)
            def _():
                z = jnp.dot(tb[...], at[:, c * CH:(c + 1) * CH], preferred_element_type=F32)
                zp[c] = z.reshape(2, 2, OWN, CH)

            d2d_z[c].start()

        def a_transpose(c):
            @pl.when(step == 0)
            def _():
                def block(b, carry):
                    blk = cols(b, BL)
                    at[blk, c * CH:(c + 1) * CH] = a[c * CH:(c + 1) * CH, blk].T
                    return carry

                lax.fori_loop(0, dim // BL, block, 0)

        def z_chip(c):
            d2d_z[c].wait_recv()
            zp[c, h] = zp[c, h] + zr1[c]
            ici_z[c].start()

        def r_own(c):
            ici_z[c].wait_recv()
            z = zp[c, h, x] + zr2[c]
            n = CH // 128
            labels = jnp.concatenate([y[c * n + i:c * n + i + 1, :] for i in range(n)], axis=1)
            r = labels.astype(F32) - jax.nn.sigmoid(z)
            rb[c, h, x] = r.astype(BF16)
            ici_r[c].start()
            d2d_r[c].start()

        def r_forward(c):
            ici_r[c].wait_recv()
            d2d_f[c].start()

        def r_all(c):
            d2d_r[c].wait_recv()
            d2d_f[c].wait_recv()

        def gram():
            ga = lax.dot_general(tb[...], tb[0:256, :], DIMS_NT, preferred_element_type=F32)
            d2 = lax.dot_general(tb[256:384, :], tb[256:384, :], DIMS_NT, preferred_element_type=F32)
            d0, d1 = ga[0:128, 0:128], ga[128:256, 128:256]
            diag = rows3([jnp.sum(jnp.where(eye, d, 0.0), axis=0, keepdims=True) for d in (d0, d1, d2)])
            packed = jnp.concatenate(
                [ga[128:256, 0:128], ga[256:384, 0:128], ga[256:384, 128:256], jnp.where(low, d0, d1),
                 jnp.where(fold, pltpu.roll(d2[64:128], 64, 1), d2[0:64])], axis=0)
            for i in range(2):
                for j in range(2):
                    q = 2 * i + j
                    pp[i, j, 0:QR, :] = packed[QR * q:QR * (q + 1)]
                    pp[i, j, QR:QR + 8, :] = diag
            d2d_p.start()

        def gram_chip():
            d2d_p.wait_recv()
            pp[h] = pp[h] + pr1[...]
            ici_p.start()

        def kern_own():
            ici_p.wait_recv()
            pq = pp[h, x] + pr2[...]
            n_row = [pq[QR + i:QR + i + 1, :] for i in range(3)]
            n_col = [to_col(n) for n in n_row]
            pair = jnp.concatenate(
                [n_col[1] + n_row[0], n_col[2] + n_row[0], n_col[2] + n_row[1],
                 jnp.where(low, n_col[0] + n_row[0], n_col[1] + n_row[1]),
                 jnp.where(fold, n_col[2][64:128] + pltpu.roll(jnp.broadcast_to(n_row[2], (64, 128)), 64, 1),
                           n_col[2][0:64] + n_row[2])], axis=0)
            ns[...] = pair.reshape(2, 2, QR, 128)
            k = jnp.exp(-(jnp.maximum(ns[h, x] - 2.0 * pq[0:QR], 0.0) * inv_h))
            k16[h, x] = k.astype(BF16)
            ici_k.start()
            d2d_k.start()
            k32[h, x] = k
            part = unpack(k32[...].reshape(4 * QR, 128), 0.0)
            ks[h, x] = rows3([jnp.sum(part[0][j] + part[1][j] + part[2][j], axis=0, keepdims=True)
                              for j in range(3)])
            ici_s.start()
            d2d_s.start()

        def kern_forward():
            ici_k.wait_recv()
            fwd_k.start()
            ici_s.wait_recv()
            fwd_s.start()

        def kern_all():
            for cp in (d2d_k, fwd_k, d2d_s, fwd_s):
                cp.wait_recv()
            kmat = unpack(k16[...].reshape(4 * QR, 128).astype(F32), 1.0)
            total = (ks[0, 0] + ks[0, 1]) + (ks[1, 0] + ks[1, 1])
            lane = lax.broadcasted_iota(jnp.int32, (1, 128), 1)
            absent = [jnp.zeros((1, 128), F32), jnp.ones((1, 128), F32), jnp.where(lane >= 64, 1.0, 0.0)]
            for i in range(3):
                r = slice(128 * i, 128 * (i + 1))
                for j in range(3):
                    kb[r, 128 * j:128 * (j + 1)] = kmat[i][j].astype(BF16)
                kb[r, 384:512] = kmat[i][2].astype(BF16)
                krow[r, :] = jnp.broadcast_to(to_col(total[i:i + 1, :] + absent[i]), (128, 128))

        def proj():
            def block(b, acc):
                blk = cols(b, BQ)
                xb = (th[:, blk] - mu[:, blk]).astype(BF16)
                return acc + lax.dot_general(xb, u[:, blk], DIMS_NT, preferred_element_type=F32)

            q = lax.fori_loop(0, dim // BQ, block, jnp.zeros((NP, 16), F32))
            qp[...] = q.T.reshape(2, 8, NP)
            d2d_q.start()

        def proj_chip():
            d2d_q.wait_recv()
            qp[h] = qp[h] + qr1[...]
            ici_q.start()

        def proj_own():
            ici_q.wait_recv()
            qf[h] = qp[h] + qr2[...]
            d2d_qg.start()

        def prior():
            d2d_qg.wait_recv()
            qb[...] = qf[...].reshape(16, NP).T.astype(BF16)

            def block(b, carry):
                blk = cols(b, BB)
                low_rank = jnp.dot(qb[...], u[:, blk], preferred_element_type=F32)
                base[:, blk] = -((th[:, blk] - mu[:, blk]) * lam[:, blk]) - low_rank
                return carry

            lax.fori_loop(0, dim // BB, block, 0)

        def pull():
            def block(b, carry):
                blk = cols(b, BK)
                t = th[:, blk]
                pulled = jnp.dot(kb[:, 0:256], tb[0:256, blk], preferred_element_type=F32)
                th[:, blk] = t + c1 * (krow[:, 0:1] * t - pulled)
                return carry

            lax.fori_loop(0, dim // BK, block, 0)

        def likelihood(c):
            r_all(c)

            def block(b, carry):
                blk = cols(b, BR)
                ra = jnp.dot(rb[c].reshape(NP, CH), a[pl.ds(c * CH, CH), blk], preferred_element_type=F32)
                base[:, blk] = base[:, blk] + beta * ra
                return carry

            lax.fori_loop(0, dim // BR, block, 0)

        def update(c):
            r_all(c)

            def block(b, carry):
                blk = cols(b, BU)
                ra = jnp.dot(rb[c].reshape(NP, CH), a[pl.ds(c * CH, CH), blk], preferred_element_type=F32)
                s = (base[:, blk] + beta * ra).astype(BF16)
                rhs = jnp.concatenate([s, tb[256:384, blk] * (-two_h)], axis=0)
                t = th[:, blk] + c2 * jnp.dot(kb[...], rhs, preferred_element_type=F32)
                th[:, blk] = t
                tb[:, blk] = t.astype(BF16)
                return carry

            lax.fori_loop(0, dim // BU, block, 0)

        z_dot(0)
        gram()
        z_chip(0)
        z_dot(1)
        gram_chip()
        z_chip(1)
        proj()
        z_dot(2)
        proj_chip()
        a_transpose(0)
        kern_own()
        z_chip(2)
        a_transpose(1)
        proj_own()
        r_own(0)
        kern_forward()
        prior()
        r_own(1)
        a_transpose(2)
        kern_all()
        r_own(2)
        r_forward(0)
        pull()
        r_forward(1)
        likelihood(0)
        r_forward(2)
        likelihood(1)
        update(2)

        for cp in d2d_z + ici_z + ici_r + d2d_r + d2d_f + [
                d2d_p, ici_p, ici_k, d2d_k, fwd_k, ici_s, d2d_s, fwd_s, d2d_q, ici_q, d2d_qg]:
            cp.wait_send()
        return carry

    lax.fori_loop(0, NUM_STEPS, step_body, 0)


def solution(mesh):
    feat_size = mesh.shape["feat"]

    def local_run(particles, prec_diag, low_factor, prior_mean, data_mat, labels):
        n_part, dim_local = particles.shape
        dim_full = dim_local * feat_size
        m_rows = data_mat.shape[0]
        band_width = 2.0 * dim_full
        step_size = dim_full / 4.0
        beta = 2.0 / math.sqrt(m_rows * dim_full)
        c1 = step_size * (2.0 / band_width) / n_part
        c2 = step_size / n_part
        nb = dim_local // BL
        vm = pltpu.VMEM
        scratch = [
            vm((1, dim_local), F32),
            vm((1, dim_local), F32),
            vm((16, dim_local), BF16),
            vm((m_rows // 128, 128), jnp.int32),
            vm((MD, dim_local), BF16),
            vm((dim_local, MD), BF16),
            vm((NP, dim_local), BF16),
            vm((NP, dim_local), F32),
            vm((NC, 2, 2, OWN, CH), F32),
            vm((NC, 2, OWN, CH), F32),
            vm((NC, OWN, CH), F32),
            vm((NC, 2, 2, OWN, CH), BF16),
            vm((2, 2, QR + 8, 128), F32),
            vm((2, QR + 8, 128), F32),
            vm((QR + 8, 128), F32),
            vm((2, 2, QR, 128), F32),
            vm((2, 2, QR, 128), F32),
            vm((2, 2, QR, 128), BF16),
            vm((2, 2, 8, 128), F32),
            vm((2, 8, NP), F32),
            vm((8, NP), F32),
            vm((8, NP), F32),
            vm((2, 8, NP), F32),
            vm((NP, NP + 128), BF16),
            vm((NP, 128), F32),
            vm((NP, 16), BF16),
            pltpu.SemaphoreType.DMA((N_SEM,)),
            pltpu.SemaphoreType.DMA((N_SEM,)),
            pltpu.SemaphoreType.DMA((nb + NC + 4,)),
        ]
        hspec = pl.BlockSpec(memory_space=pltpu.HBM)
        vspec = pl.BlockSpec(memory_space=pltpu.VMEM)
        return pl.pallas_call(
            functools.partial(kernel, beta, c1, c2, 2.0 / band_width, 1.0 / band_width),
            out_shape=pltpu.VMEM((n_part, dim_local), F32),
            in_specs=[hspec] * 6,
            out_specs=vspec,
            scratch_shapes=scratch,
            compiler_params=pltpu.CompilerParams(
                collective_id=0, has_side_effects=True, vmem_limit_bytes=60_000_000),
            name="svgd",
        )(particles, prec_diag.reshape(1, dim_local), prior_mean.reshape(1, dim_local), low_factor.T,
          data_mat, labels.reshape(m_rows // 128, 128))

    return jax.shard_map(
        local_run,
        mesh=mesh,
        in_specs=(P("ens", "feat"), P(("ens", "feat")), P(("ens", "feat"), None),
                  P(("ens", "feat")), P("ens", "feat"), P("ens")),
        out_specs=P("ens", "feat"),
        check_vma=False,
    )
```

time: 288 us -> 73 us (0.25)
  matrix products: 136 us -> 0 us
  Pallas kernels: 0 us -> 70.2 us
  waiting for transfers between devices: 67.7 us -> 0 us
  blocking collectives: 54.8 us -> 0 us
  between operations: 13.3 us -> 0.01 us
  local copies, waits for them, and re-layouts: 13.4 us -> 2.71 us
    dot_general x18 -> x0, matrix products: 136 us -> none  [the longest x3 31.1 us: local_run(): jnp.dot(kern_bf, log_grad.astype(jnp.bfloat16), preferred_element_type=jn...]
    pallas_call x0 -> x1, Pallas kernels: none -> 70.2 us  [local_run(): pl.pallas_call(functools.partial(kernel, beta, c1, c2, 2.0 / band_width,...]
    psum x3 -> x0, waiting for transfers between devices: 67.7 us -> none  [local_run(): lax.psum(lax.dot_general(part_bf, data_mat, DIMS_NT, preferred_element_ty...]
    psum x3 -> x0, blocking collectives: 54.8 us -> none  [local_run(): lax.psum(jnp.dot(centred.astype(jnp.bfloat16), low_factor, preferred_elem...]
    gather x3 -> x0, local copies, waits for them, and re-layouts: 13.3 us -> none  [local_run(): sq_norm = jnp.diagonal(gram_mat)]
  transfers between devices with their start and end apart: 3 -> 0, of which waited for: 3 -> 0; matrix products, arithmetic and copies ran while one was open for 4% -> 0% of each run, Pallas kernels for 0% -> 0%
where the time goes in v2:
time: 73 us; the launch traced here: 72.9 us
  Pallas kernels  70.2 us (96%)
  local copies, waits for them, and re-layouts  2.71 us (4%)
    pallas_call x1, Pallas kernels, local_run(): pl.pallas_call(functools.partial(kernel, beta, c1, c2, 2.0 / band_width,...  70.2 us
    unnamed x1, local copies, waits for them, and re-layouts  2.71 us

profile of v2, /device:TPU:0, one launch (start us, length us, event | category | flops | bytes accessed | tf_op | source)
XLA Modules:
  0.0 72.9 jit_solution(5431832855066406129)
XLA Ops:
  0.0 70.2 %svgd.1 = f32[384,4096]{1,0:T(8,128)S(1)} custom-call(f32[384,4096]{1,0:T(8,128)} %th_hbm.1, f32[1,4096]{1,0:T(1,128)} %bitcast.5, f32[1,4096]{1,0:T(1,128)} %bitcast.6, bf16[16,4096]{1,0:T(8,128)(2,1)} %bitcast.4, bf16[768,4096]{1,0:T(8,128)(2,1)} %a_hbm.1, s32[6,128]{1,0:T(8,128)} %bitcast.7), custom_call_target="tpu_custom_call" | custom-call | tf_op jit(solution)/shard_map/svgd/pallas_call | solution.py:390
  70.2 2.7 %copy.8 = f32[384,4096]{1,0:T(8,128)} copy(f32[384,4096]{1,0:T(8,128)S(1)} %svgd.1) | data formatting | bytes 12582912

commit v3 on v2

--- a/solution.py
+++ b/solution.py
@@ -26,6 +26,9 @@
 BK = 4096
 BR = 4096
 BU = 4096
+BO = 512
+
+VMEM_STEPS = 43_000_000
 
 D2D_Z, ICI_Z, ICI_R, D2D_R, D2D_F = 0, NC, 2 * NC, 3 * NC, 4 * NC
 (D2D_P, ICI_P, ICI_K, D2D_K, FWD_K, ICI_S, D2D_S, FWD_S,
@@ -33,9 +36,32 @@
 N_SEM = 5 * NC + 11
 
 
-def kernel(beta, c1, c2, two_h, inv_h, th_hbm, lam_hbm, mu_hbm, u_hbm, a_hbm, y_hbm, th,
-           lam, mu, u, y, a, at, tb, base, zp, zr1, zr2, rb, pp, pr1, pr2, ns, k32, k16, ks, qp, qr1, qr2, qf,
-           kb, krow, qb, ss, rs, ls):
+def chip_rows(chip):
+    return pl.ds(pl.multiple_of(2 * OWN * chip, 2 * OWN), 2 * OWN)
+
+
+def drive(beta, c2, two_h, th, base, a, tb, rb, c, chip, kx, j0, blk):
+    ra = jnp.dot(rb[c, chip].reshape(2 * OWN, CH), a[pl.ds(c * CH, CH), blk], preferred_element_type=F32)
+    s = (base[chip_rows(chip), blk] + beta * ra).astype(BF16)
+    rhs = jnp.concatenate([s, tb[j0:j0 + 64, blk] * (-two_h)], axis=0)
+    return th[:, blk] + c2 * jnp.dot(kx[...], rhs, preferred_element_type=F32)
+
+
+def last_kernel(beta, c2, two_h, th, base, a, tb, rb, kb, out_hbm, out, sems):
+    ox = 1 - lax.div(lax.axis_index("feat"), 2)
+    copies = []
+    for b in range(th.shape[1] // BO):
+        blk = pl.ds(b * BO, BO)
+        out[:, blk] = drive(beta, c2, two_h, th, base, a, tb, rb, NC - 1, ox, kb, 320, blk)
+        copies.append(pltpu.make_async_copy(out.at[:, blk], out_hbm.at[:, blk], sems.at[b]))
+        copies[-1].start()
+    for cp in copies:
+        cp.wait()
+
+
+def kernel(beta, c1, c2, two_h, inv_h, th_hbm, lam_hbm, mu_hbm, u_hbm, a_hbm, y_hbm, th, base, a, tb, rb, kb,
+           lam, mu, u, y, at, zp, zr1, zr2, pp, pr1, pr2, ns, k32, k16, ks, qp, qr1, qr2, qf,
+           ka, kp, krow, qb, ss, rs, ls):
     dim = th.shape[1]
     nb = dim // BL
     me = lax.axis_index("feat")
@@ -86,7 +112,7 @@
 
     ri = lax.broadcasted_iota(jnp.int32, (128, 128), 0)
     ci = lax.broadcasted_iota(jnp.int32, (128, 128), 1)
-    eye, low = ri == ci, ri >= ci
+    eye, low, half = ri == ci, ri >= ci, ci < 64
     r64 = lax.broadcasted_iota(jnp.int32, (64, 128), 0)
     c64 = lax.broadcasted_iota(jnp.int32, (64, 128), 1)
     fold = (c64 < 64) & (r64 < c64)
@@ -109,11 +135,11 @@
         return [[d0, m10.T, m20.T], [m10, d1, m21.T], [m20, m21, d2]]
 
     def step_body(step, carry):
-        d2d_z = [remote(zp.at[c, oh], zr1.at[c], D2D_Z + c, partner) for c in range(NC)]
-        ici_z = [remote(zp.at[c, h, ox], zr2.at[c], ICI_Z + c, cross) for c in range(NC)]
-        ici_r = [remote(rb.at[c, h, x], rb.at[c, h, x], ICI_R + c, cross) for c in range(NC)]
-        d2d_r = [remote(rb.at[c, h, x], rb.at[c, h, x], D2D_R + c, partner) for c in range(NC)]
-        d2d_f = [remote(rb.at[c, h, ox], rb.at[c, h, ox], D2D_F + c, partner) for c in range(NC)]
+        d2d_z = [remote(zp.at[c, :, oh], zr1.at[c], D2D_Z + c, partner) for c in range(NC)]
+        ici_z = [remote(zp.at[c, ox, h], zr2.at[c], ICI_Z + c, cross) for c in range(NC)]
+        ici_r = [remote(rb.at[c, x, h], rb.at[c, x, h], ICI_R + c, cross) for c in range(NC)]
+        d2d_r = [remote(rb.at[c, x, h], rb.at[c, x, h], D2D_R + c, partner) for c in range(NC)]
+        d2d_f = [remote(rb.at[c, ox, h], rb.at[c, ox, h], D2D_F + c, partner) for c in range(NC)]
         d2d_p = remote(pp.at[oh], pr1, D2D_P, partner)
         ici_p = remote(pp.at[h, ox], pr2, ICI_P, cross)
         ici_k = remote(k16.at[h, x], k16.at[h, x], ICI_K, cross)
@@ -140,6 +166,27 @@
 
             d2d_z[c].start()
 
+        def z_dot_first(c):
+            def rows(i):
+                return jnp.concatenate([tb[pl.ds(pl.multiple_of((2 * j + i) * OWN, OWN), OWN), :] for j in range(2)], axis=0)
+
+            @pl.when(step == 0)
+            def _():
+                a_load(c).wait()
+                zp[c, :, oh] = lax.dot_general(rows(oh), a[pl.ds(c * CH, CH), :], DIMS_NT,
+                                               preferred_element_type=F32).reshape(2, OWN, CH)
+                d2d_z[c].start()
+                zp[c, :, h] = lax.dot_general(rows(h), a[pl.ds(c * CH, CH), :], DIMS_NT,
+                                              preferred_element_type=F32).reshape(2, OWN, CH)
+
+            @pl.when(step > 0)
+            def _():
+                zp[c, :, oh] = jnp.dot(rows(oh), at[:, c * CH:(c + 1) * CH],
+                                       preferred_element_type=F32).reshape(2, OWN, CH)
+                d2d_z[c].start()
+                zp[c, :, h] = jnp.dot(rows(h), at[:, c * CH:(c + 1) * CH],
+                                      preferred_element_type=F32).reshape(2, OWN, CH)
+
         def a_transpose(c):
             @pl.when(step == 0)
             def _():
@@ -152,26 +199,22 @@
 
         def z_chip(c):
             d2d_z[c].wait_recv()
-            zp[c, h] = zp[c, h] + zr1[c]
+            zp[c, :, h] = zp[c, :, h] + zr1[c]
             ici_z[c].start()
 
         def r_own(c):
             ici_z[c].wait_recv()
-            z = zp[c, h, x] + zr2[c]
+            z = zp[c, x, h] + zr2[c]
             n = CH // 128
             labels = jnp.concatenate([y[c * n + i:c * n + i + 1, :] for i in range(n)], axis=1)
             r = labels.astype(F32) - jax.nn.sigmoid(z)
-            rb[c, h, x] = r.astype(BF16)
+            rb[c, x, h] = r.astype(BF16)
             ici_r[c].start()
             d2d_r[c].start()
 
         def r_forward(c):
             ici_r[c].wait_recv()
             d2d_f[c].start()
-
-        def r_all(c):
-            d2d_r[c].wait_recv()
-            d2d_f[c].wait_recv()
 
         def gram():
             ga = lax.dot_general(tb[...], tb[0:256, :], DIMS_NT, preferred_element_type=F32)
@@ -230,9 +273,14 @@
             absent = [jnp.zeros((1, 128), F32), jnp.ones((1, 128), F32), jnp.where(lane >= 64, 1.0, 0.0)]
             for i in range(3):
                 r = slice(128 * i, 128 * (i + 1))
-                for j in range(3):
-                    kb[r, 128 * j:128 * (j + 1)] = kmat[i][j].astype(BF16)
-                kb[r, 384:512] = kmat[i][2].astype(BF16)
+                k0, k1, k2 = kmat[i]
+                s1, s2 = pltpu.roll(k1, 64, 1), pltpu.roll(k2, 64, 1)
+                first = x == 0
+                ka[r, :] = jnp.where(first, jnp.concatenate([k0, jnp.where(half, k1, s2)], axis=1),
+                                     jnp.concatenate([jnp.where(half, s1, s2), s2], axis=1)).astype(BF16)
+                kb[r, :] = jnp.where(first, jnp.concatenate([jnp.where(half, s1, s2), jnp.where(half, s2, k2)], axis=1),
+                                     jnp.concatenate([k0, jnp.where(half, k1, k2)], axis=1)).astype(BF16)
+                kp[r, :] = jnp.concatenate([k0, k1], axis=1).astype(BF16)
                 krow[r, :] = jnp.broadcast_to(to_col(total[i:i + 1, :] + absent[i]), (128, 128))
 
         def proj():
@@ -271,66 +319,86 @@
             def block(b, carry):
                 blk = cols(b, BK)
                 t = th[:, blk]
-                pulled = jnp.dot(kb[:, 0:256], tb[0:256, blk], preferred_element_type=F32)
+                pulled = jnp.dot(kp[...], tb[0:256, blk], preferred_element_type=F32)
                 th[:, blk] = t + c1 * (krow[:, 0:1] * t - pulled)
                 return carry
 
             lax.fori_loop(0, dim // BK, block, 0)
 
-        def likelihood(c):
-            r_all(c)
+        def likelihood(c, chip):
+            rows = chip_rows(chip)
 
             def block(b, carry):
                 blk = cols(b, BR)
-                ra = jnp.dot(rb[c].reshape(NP, CH), a[pl.ds(c * CH, CH), blk], preferred_element_type=F32)
-                base[:, blk] = base[:, blk] + beta * ra
+                ra = jnp.dot(rb[c, chip].reshape(2 * OWN, CH), a[pl.ds(c * CH, CH), blk], preferred_element_type=F32)
+                base[rows, blk] = base[rows, blk] + beta * ra
                 return carry
 
             lax.fori_loop(0, dim // BR, block, 0)
 
-        def update(c):
-            r_all(c)
+        def likelihood_near(c):
+            d2d_r[c].wait_recv()
+            likelihood(c, x)
+
+        def likelihood_far(c):
+            d2d_f[c].wait_recv()
+            likelihood(c, ox)
+
+        def update_near(c):
+            d2d_r[c].wait_recv()
 
             def block(b, carry):
                 blk = cols(b, BU)
-                ra = jnp.dot(rb[c].reshape(NP, CH), a[pl.ds(c * CH, CH), blk], preferred_element_type=F32)
-                s = (base[:, blk] + beta * ra).astype(BF16)
-                rhs = jnp.concatenate([s, tb[256:384, blk] * (-two_h)], axis=0)
-                t = th[:, blk] + c2 * jnp.dot(kb[...], rhs, preferred_element_type=F32)
+                th[:, blk] = drive(beta, c2, two_h, th, base, a, tb, rb, c, x, ka, 256, blk)
+                return carry
+
+            lax.fori_loop(0, dim // BU, block, 0)
+
+        def update_far(c):
+            d2d_f[c].wait_recv()
+
+            def block(b, carry):
+                blk = cols(b, BU)
+                t = drive(beta, c2, two_h, th, base, a, tb, rb, c, ox, kb, 320, blk)
                 th[:, blk] = t
                 tb[:, blk] = t.astype(BF16)
                 return carry
 
-            lax.fori_loop(0, dim // BU, block, 0)
+            @pl.when(step < NUM_STEPS - 1)
+            def _():
+                lax.fori_loop(0, dim // BU, block, 0)
 
         z_dot(0)
         gram()
         z_chip(0)
         z_dot(1)
+        proj()
         gram_chip()
+        proj_chip()
         z_chip(1)
-        proj()
         z_dot(2)
-        proj_chip()
         a_transpose(0)
         kern_own()
+        proj_own()
+        a_transpose(1)
         z_chip(2)
-        a_transpose(1)
-        proj_own()
         r_own(0)
-        kern_forward()
         prior()
         r_own(1)
         a_transpose(2)
+        kern_forward()
+        likelihood_near(0)
+        likelihood_near(1)
         kern_all()
         r_own(2)
+        pull()
         r_forward(0)
-        pull()
+        update_near(2)
         r_forward(1)
-        likelihood(0)
         r_forward(2)
-        likelihood(1)
-        update(2)
+        likelihood_far(0)
+        likelihood_far(1)
+        update_far(2)
 
         for cp in d2d_z + ici_z + ici_r + d2d_r + d2d_f + [
                 d2d_p, ici_p, ici_k, d2d_k, fwd_k, ici_s, d2d_s, fwd_s, d2d_q, ici_q, d2d_qg]:
@@ -359,14 +427,10 @@
             vm((1, dim_local), F32),
             vm((16, dim_local), BF16),
             vm((m_rows // 128, 128), jnp.int32),
-            vm((MD, dim_local), BF16),
             vm((dim_local, MD), BF16),
-            vm((NP, dim_local), BF16),
-            vm((NP, dim_local), F32),
             vm((NC, 2, 2, OWN, CH), F32),
             vm((NC, 2, OWN, CH), F32),
             vm((NC, OWN, CH), F32),
-            vm((NC, 2, 2, OWN, CH), BF16),
             vm((2, 2, QR + 8, 128), F32),
             vm((2, QR + 8, 128), F32),
             vm((QR + 8, 128), F32),
@@ -378,7 +442,8 @@
             vm((8, NP), F32),
             vm((8, NP), F32),
             vm((2, 8, NP), F32),
-            vm((NP, NP + 128), BF16),
+            vm((NP, 256), BF16),
+            vm((NP, 256), BF16),
             vm((NP, 128), F32),
             vm((NP, 16), BF16),
             pltpu.SemaphoreType.DMA((N_SEM,)),
@@ -387,17 +452,33 @@
         ]
         hspec = pl.BlockSpec(memory_space=pltpu.HBM)
         vspec = pl.BlockSpec(memory_space=pltpu.VMEM)
-        return pl.pallas_call(
+        kept = pl.pallas_call(
             functools.partial(kernel, beta, c1, c2, 2.0 / band_width, 1.0 / band_width),
-            out_shape=pltpu.VMEM((n_part, dim_local), F32),
+            out_shape=[
+                vm((n_part, dim_local), F32),
+                vm((n_part, dim_local), F32),
+                vm((m_rows, dim_local), BF16),
+                vm((n_part, dim_local), BF16),
+                vm((NC, 2, 2, OWN, CH), BF16),
+                vm((n_part, 256), BF16),
+            ],
             in_specs=[hspec] * 6,
-            out_specs=vspec,
+            out_specs=[vspec] * 6,
             scratch_shapes=scratch,
             compiler_params=pltpu.CompilerParams(
-                collective_id=0, has_side_effects=True, vmem_limit_bytes=60_000_000),
+                collective_id=0, has_side_effects=True, vmem_limit_bytes=VMEM_STEPS),
             name="svgd",
         )(particles, prec_diag.reshape(1, dim_local), prior_mean.reshape(1, dim_local), low_factor.T,
           data_mat, labels.reshape(m_rows // 128, 128))
+        return pl.pallas_call(
+            functools.partial(last_kernel, beta, c2, 2.0 / band_width),
+            out_shape=jax.ShapeDtypeStruct((n_part, dim_local), F32),
+            in_specs=[vspec] * 6,
+            out_specs=hspec,
+            scratch_shapes=[vm((n_part, dim_local), F32), pltpu.SemaphoreType.DMA((dim_local // BO,))],
+            compiler_params=pltpu.CompilerParams(vmem_limit_bytes=12 * 1024 * 1024),
+            name="svgd_last",
+        )(*kept)
 
     return jax.shard_map(
         local_run,

time: 73 us -> 69.2 us (0.948)
  local copies, waits for them, and re-layouts: 2.71 us -> 0 us
  Pallas kernels: 70.2 us -> 69.1 us
    pallas_call x1, Pallas kernels: 70.2 us -> 65.6 us  [local_run(): pl.pallas_call(functools.partial(kernel, beta, c1, c2, 2.0 / band_width,...]
    pallas_call x0 -> x1, Pallas kernels: none -> 3.49 us  [local_run(): pl.pallas_call(functools.partial(last_kernel, beta, c2, 2.0 / band_width)...]
    unnamed x1 -> x0, local copies, waits for them, and re-layouts: 2.71 us -> none
where the time goes in v3:
time: 69.2 us; the launch traced here: 69.1 us
  Pallas kernels  69.1 us (100%)
    pallas_call x1, Pallas kernels, local_run(): pl.pallas_call(functools.partial(kernel, beta, c1, c2, 2.0 / band_width,...  65.6 us
    pallas_call x1, Pallas kernels, local_run(): pl.pallas_call(functools.partial(last_kernel, beta, c2, 2.0 / band_width)...  3.49 us

profile of v3, /device:TPU:0, one launch (start us, length us, event | category | flops | bytes accessed | tf_op | source)
XLA Modules:
  0.0 69.1 jit_solution(16705852321407541632)
XLA Ops:
  0.0 65.6 %svgd.1 = (f32[384,4096]{1,0:T(8,128)S(1)}, f32[384,4096]{1,0:T(8,128)S(1)}, bf16[768,4096]{1,0:T(8,128)(2,1)S(1)}, bf16[384,4096]{1,0:T(8,128)(2,1)S(1)}, bf16[...) custom-call(f32[384,4096]{1,0:T(8,128)} %th_hbm.1, f32[1,4096]{1,0:T(1,128)} %bitcast.5, ...), custom_call_target="tpu_custom_call" | custom-call | tf_op jit(solution)/shard_map/svgd/pallas_call | solution.py:455
  65.6 3.5 %svgd_last.1 = f32[384,4096]{1,0:T(8,128)} custom-call(f32[384,4096]{1,0:T(8,128)S(1)} %get-tuple-element.11.th, f32[384,4096]{1,0:T(8,128)S(1)} %get-tuple-element.12.base, bf16[768,4096]{1,0:T(8,128)(2,1)S(1)} %get-tuple-element.13.a, bf16[384,4096]{1,0:T(8,128)(2,1)S(1)} %get-tuple-element.14.tb, bf16[3,2,2,96,256]{4,3,2,1,0:T(8,128)(2,1)S(1)} %get-tuple-element.15.rb, ...), custom_call_target="tpu_custom_call" | custom-call | tf_op jit(solution)/shard_map/svgd_last/pallas_call | solution.py:473

commit v4 on v3

--- a/solution.py
+++ b/solution.py
@@ -26,7 +26,8 @@
 BK = 4096
 BR = 4096
 BU = 4096
-BO = 512
+NF = 4
+BO = 1024
 
 VMEM_STEPS = 43_000_000
 
@@ -87,10 +88,14 @@
 
     small = [pltpu.make_async_copy(src, dst, ls.at[nb + NC + i])
              for i, (src, dst) in enumerate([(lam_hbm, lam), (mu_hbm, mu), (u_hbm, u), (y_hbm, y)])]
-    for b in range(nb):
-        th_load(b).start()
-    for c in range(NC):
-        a_load(c).start()
+    def a_first(i):
+        part = pl.ds(i * (dim // NF), dim // NF)
+        return pltpu.make_async_copy(a_hbm.at[pl.ds(0, CH), part], a.at[pl.ds(0, CH), part], ls.at[nb + NC + 4 + i])
+
+    for i in range(NF):
+        for b in range(i * nb // NF, (i + 1) * nb // NF):
+            th_load(b).start()
+        a_first(i).start()
     for cp in small:
         cp.start()
 
@@ -106,7 +111,15 @@
         tb[:, cols(b, BL)] = th[:, cols(b, BL)].astype(BF16)
         return carry
 
-    lax.fori_loop(0, nb, conv, 0)
+    for i in range(NF):
+        part = slice(i * (dim // NF), (i + 1) * (dim // NF))
+        lax.fori_loop(i * nb // NF, (i + 1) * nb // NF, conv, 0)
+        a_first(i).wait()
+        if i == NF - 1:
+            for c in range(1, NC):
+                a_load(c).start()
+        z = lax.dot_general(tb[:, part], a[0:CH, part], DIMS_NT, preferred_element_type=F32).reshape(2, 2, OWN, CH)
+        zp[0] = z if i == 0 else zp[0] + z
     for cp in small:
         cp.wait()
 
@@ -153,11 +166,12 @@
         d2d_qg = remote(qf.at[h], qf.at[h], D2D_QG, partner)
 
         def z_dot(c):
-            @pl.when(step == 0)
-            def _():
-                a_load(c).wait()
-                z = lax.dot_general(tb[...], a[pl.ds(c * CH, CH), :], DIMS_NT, preferred_element_type=F32)
-                zp[c] = z.reshape(2, 2, OWN, CH)
+            if c > 0:
+                @pl.when(step == 0)
+                def _():
+                    a_load(c).wait()
+                    z = lax.dot_general(tb[...], a[pl.ds(c * CH, CH), :], DIMS_NT, preferred_element_type=F32)
+                    zp[c] = z.reshape(2, 2, OWN, CH)
 
             @pl.when(step > 0)
             def _():
@@ -165,27 +179,6 @@
                 zp[c] = z.reshape(2, 2, OWN, CH)
 
             d2d_z[c].start()
-
-        def z_dot_first(c):
-            def rows(i):
-                return jnp.concatenate([tb[pl.ds(pl.multiple_of((2 * j + i) * OWN, OWN), OWN), :] for j in range(2)], axis=0)
-
-            @pl.when(step == 0)
-            def _():
-                a_load(c).wait()
-                zp[c, :, oh] = lax.dot_general(rows(oh), a[pl.ds(c * CH, CH), :], DIMS_NT,
-                                               preferred_element_type=F32).reshape(2, OWN, CH)
-                d2d_z[c].start()
-                zp[c, :, h] = lax.dot_general(rows(h), a[pl.ds(c * CH, CH), :], DIMS_NT,
-                                              preferred_element_type=F32).reshape(2, OWN, CH)
-
-            @pl.when(step > 0)
-            def _():
-                zp[c, :, oh] = jnp.dot(rows(oh), at[:, c * CH:(c + 1) * CH],
-                                       preferred_element_type=F32).reshape(2, OWN, CH)
-                d2d_z[c].start()
-                zp[c, :, h] = jnp.dot(rows(h), at[:, c * CH:(c + 1) * CH],
-                                      preferred_element_type=F32).reshape(2, OWN, CH)
 
         def a_transpose(c):
             @pl.when(step == 0)
@@ -448,7 +441,7 @@
             vm((NP, 16), BF16),
             pltpu.SemaphoreType.DMA((N_SEM,)),
             pltpu.SemaphoreType.DMA((N_SEM,)),
-            pltpu.SemaphoreType.DMA((nb + NC + 4,)),
+            pltpu.SemaphoreType.DMA((nb + NC + 4 + NF,)),
         ]
         hspec = pl.BlockSpec(memory_space=pltpu.HBM)
         vspec = pl.BlockSpec(memory_space=pltpu.VMEM)

time: 69.2 us -> 67.5 us (0.975)
  Pallas kernels: 69.1 us -> 67.4 us
    pallas_call x1, Pallas kernels: 65.6 us -> 64.1 us  [local_run(): pl.pallas_call(functools.partial(kernel, beta, c1, c2, 2.0 / band_width,...]
where the time goes in v4:
time: 67.5 us; the launch traced here: 67.4 us
  Pallas kernels  67.4 us (100%)
    pallas_call x1, Pallas kernels, local_run(): pl.pallas_call(functools.partial(kernel, beta, c1, c2, 2.0 / band_width,...  64.1 us
    pallas_call x1, Pallas kernels, local_run(): pl.pallas_call(functools.partial(last_kernel, beta, c2, 2.0 / band_width)...  3.33 us

profile of v4, /device:TPU:0, one launch (start us, length us, event | category | flops | bytes accessed | tf_op | source)
XLA Modules:
  0.0 67.4 jit_solution(6013096857809573576)
XLA Ops:
  0.0 64.1 %svgd.1 = (f32[384,4096]{1,0:T(8,128)S(1)}, f32[384,4096]{1,0:T(8,128)S(1)}, bf16[768,4096]{1,0:T(8,128)(2,1)S(1)}, bf16[384,4096]{1,0:T(8,128)(2,1)S(1)}, bf16[...) custom-call(f32[384,4096]{1,0:T(8,128)} %th_hbm.1, f32[1,4096]{1,0:T(1,128)} %bitcast.5, ...), custom_call_target="tpu_custom_call" | custom-call | tf_op jit(solution)/shard_map/svgd/pallas_call | solution.py:448
  64.1 3.3 %svgd_last.1 = f32[384,4096]{1,0:T(8,128)} custom-call(f32[384,4096]{1,0:T(8,128)S(1)} %get-tuple-element.11.th, f32[384,4096]{1,0:T(8,128)S(1)} %get-tuple-element.12.base, bf16[768,4096]{1,0:T(8,128)(2,1)S(1)} %get-tuple-element.13.a, bf16[384,4096]{1,0:T(8,128)(2,1)S(1)} %get-tuple-element.14.tb, bf16[3,2,2,96,256]{4,3,2,1,0:T(8,128)(2,1)S(1)} %get-tuple-element.15.rb, ...), custom_call_target="tpu_custom_call" | custom-call | tf_op jit(solution)/shard_map/svgd_last/pallas_call | solution.py:466

commit v5 on v4

--- a/solution.py
+++ b/solution.py
@@ -22,7 +22,7 @@
 QR = 144
 BL = 512
 BQ = 4096
-BB = 4096
+BB = 2048
 BK = 4096
 BR = 4096
 BU = 4096
@@ -68,7 +68,7 @@
     me = lax.axis_index("feat")
     x, core = lax.div(me, 2), lax.rem(me, 2)
     ox, oc = 1 - x, 1 - core
-    partner, cross = x * 2 + oc, ox * 2 + oc
+    partner, cross, peer = x * 2 + oc, ox * 2 + oc, ox * 2 + core
     h = lax.rem(x + core, 2)
     oh = 1 - h
 
@@ -100,9 +100,9 @@
         cp.start()
 
     barrier = pltpu.get_barrier_semaphore()
-    for dev in (partner, cross):
+    for dev in (partner, cross, peer):
         pl.semaphore_signal(barrier, inc=1, device_id={"feat": dev}, device_id_type=MESH)
-    pl.semaphore_wait(barrier, 2)
+    pl.semaphore_wait(barrier, 3)
 
     k32[...] = jnp.zeros_like(k32)
 
@@ -152,7 +152,8 @@
         ici_z = [remote(zp.at[c, ox, h], zr2.at[c], ICI_Z + c, cross) for c in range(NC)]
         ici_r = [remote(rb.at[c, x, h], rb.at[c, x, h], ICI_R + c, cross) for c in range(NC)]
         d2d_r = [remote(rb.at[c, x, h], rb.at[c, x, h], D2D_R + c, partner) for c in range(NC)]
-        d2d_f = [remote(rb.at[c, ox, h], rb.at[c, ox, h], D2D_F + c, partner) for c in range(NC)]
+        d2d_f = [remote(rb.at[c, ox, h], rb.at[c, ox, h], D2D_F + c, partner) for c in range(NC - 1)]
+        ici_b = remote(rb.at[NC - 1, x, h], rb.at[NC - 1, x, h], D2D_F + NC - 1, peer)
         d2d_p = remote(pp.at[oh], pr1, D2D_P, partner)
         ici_p = remote(pp.at[h, ox], pr2, ICI_P, cross)
         ici_k = remote(k16.at[h, x], k16.at[h, x], ICI_K, cross)
@@ -202,6 +203,8 @@
             labels = jnp.concatenate([y[c * n + i:c * n + i + 1, :] for i in range(n)], axis=1)
             r = labels.astype(F32) - jax.nn.sigmoid(z)
             rb[c, x, h] = r.astype(BF16)
+            if c == NC - 1:
+                ici_b.start()
             ici_r[c].start()
             d2d_r[c].start()
 
@@ -348,7 +351,8 @@
             lax.fori_loop(0, dim // BU, block, 0)
 
         def update_far(c):
-            d2d_f[c].wait_recv()
+            ici_r[c].wait_recv()
+            ici_b.wait_recv()
 
             def block(b, carry):
                 blk = cols(b, BU)
@@ -372,15 +376,15 @@
         z_dot(2)
         a_transpose(0)
         kern_own()
+        z_chip(2)
         proj_own()
         a_transpose(1)
-        z_chip(2)
         r_own(0)
         prior()
         r_own(1)
         a_transpose(2)
+        likelihood_near(0)
         kern_forward()
-        likelihood_near(0)
         likelihood_near(1)
         kern_all()
         r_own(2)
@@ -388,13 +392,12 @@
         r_forward(0)
         update_near(2)
         r_forward(1)
-        r_forward(2)
         likelihood_far(0)
         likelihood_far(1)
         update_far(2)
 
         for cp in d2d_z + ici_z + ici_r + d2d_r + d2d_f + [
-                d2d_p, ici_p, ici_k, d2d_k, fwd_k, ici_s, d2d_s, fwd_s, d2d_q, ici_q, d2d_qg]:
+                ici_b, d2d_p, ici_p, ici_k, d2d_k, fwd_k, ici_s, d2d_s, fwd_s, d2d_q, ici_q, d2d_qg]:
             cp.wait_send()
         return carry
 

time: 67.5 us -> 67.4 us (level)
  no operation moved by 1% of the time
where the time goes in v5:
time: 67.4 us; the launch traced here: 67.3 us
  Pallas kernels  67.3 us (100%)
    pallas_call x1, Pallas kernels, local_run(): pl.pallas_call(functools.partial(kernel, beta, c1, c2, 2.0 / band_width,...  63.9 us
    pallas_call x1, Pallas kernels, local_run(): pl.pallas_call(functools.partial(last_kernel, beta, c2, 2.0 / band_width)...  3.33 us

profile of v5, /device:TPU:0, one launch (start us, length us, event | category | flops | bytes accessed | tf_op | source)
XLA Modules:
  0.0 67.3 jit_solution(17479531627673750838)
XLA Ops:
  0.0 63.9 %svgd.1 = (f32[384,4096]{1,0:T(8,128)S(1)}, f32[384,4096]{1,0:T(8,128)S(1)}, bf16[768,4096]{1,0:T(8,128)(2,1)S(1)}, bf16[384,4096]{1,0:T(8,128)(2,1)S(1)}, bf16[...) custom-call(f32[384,4096]{1,0:T(8,128)} %th_hbm.1, f32[1,4096]{1,0:T(1,128)} %bitcast.5, ...), custom_call_target="tpu_custom_call" | custom-call | tf_op jit(solution)/shard_map/svgd/pallas_call | solution.py:451
  63.9 3.3 %svgd_last.1 = f32[384,4096]{1,0:T(8,128)} custom-call(f32[384,4096]{1,0:T(8,128)S(1)} %get-tuple-element.11.th, f32[384,4096]{1,0:T(8,128)S(1)} %get-tuple-element.12.base, bf16[768,4096]{1,0:T(8,128)(2,1)S(1)} %get-tuple-element.13.a, bf16[384,4096]{1,0:T(8,128)(2,1)S(1)} %get-tuple-element.14.tb, bf16[3,2,2,96,256]{4,3,2,1,0:T(8,128)(2,1)S(1)} %get-tuple-element.15.rb, ...), custom_call_target="tpu_custom_call" | custom-call | tf_op jit(solution)/shard_map/svgd_last/pallas_call | solution.py:469

commit v6 on v5

--- a/solution.py
+++ b/solution.py
@@ -203,9 +203,9 @@
             labels = jnp.concatenate([y[c * n + i:c * n + i + 1, :] for i in range(n)], axis=1)
             r = labels.astype(F32) - jax.nn.sigmoid(z)
             rb[c, x, h] = r.astype(BF16)
+            ici_r[c].start()
             if c == NC - 1:
                 ici_b.start()
-            ici_r[c].start()
             d2d_r[c].start()
 
         def r_forward(c):

time: 67.4 us -> 67.4 us (level)
  no operation moved by 1% of the time
where the time goes in v6:
time: 67.4 us; the launch traced here: 67.3 us
  Pallas kernels  67.3 us (100%)
    pallas_call x1, Pallas kernels, local_run(): pl.pallas_call(functools.partial(kernel, beta, c1, c2, 2.0 / band_width,...  63.9 us
    pallas_call x1, Pallas kernels, local_run(): pl.pallas_call(functools.partial(last_kernel, beta, c2, 2.0 / band_width)...  3.33 us

profile of v6, /device:TPU:0, one launch (start us, length us, event | category | flops | bytes accessed | tf_op | source)
XLA Modules:
  0.0 67.3 jit_solution(1831107352904015903)
XLA Ops:
  0.0 63.9 %svgd.1 = (f32[384,4096]{1,0:T(8,128)S(1)}, f32[384,4096]{1,0:T(8,128)S(1)}, bf16[768,4096]{1,0:T(8,128)(2,1)S(1)}, bf16[384,4096]{1,0:T(8,128)(2,1)S(1)}, bf16[...) custom-call(f32[384,4096]{1,0:T(8,128)} %th_hbm.1, f32[1,4096]{1,0:T(1,128)} %bitcast.5, ...), custom_call_target="tpu_custom_call" | custom-call | tf_op jit(solution)/shard_map/svgd/pallas_call | solution.py:451
  63.9 3.3 %svgd_last.1 = f32[384,4096]{1,0:T(8,128)} custom-call(f32[384,4096]{1,0:T(8,128)S(1)} %get-tuple-element.11.th, f32[384,4096]{1,0:T(8,128)S(1)} %get-tuple-element.12.base, bf16[768,4096]{1,0:T(8,128)(2,1)S(1)} %get-tuple-element.13.a, bf16[384,4096]{1,0:T(8,128)(2,1)S(1)} %get-tuple-element.14.tb, bf16[3,2,2,96,256]{4,3,2,1,0:T(8,128)(2,1)S(1)} %get-tuple-element.15.rb, ...), custom_call_target="tpu_custom_call" | custom-call | tf_op jit(solution)/shard_map/svgd_last/pallas_call | solution.py:469
